TPU v7x, 32 devices: a whole 2x2x4 slice. The times are simulated.
32 devices in a mesh: sector: 8 (over y, x, core), row: 4 (over z).
Axes of the slice: x: 2, y: 2, z: 4, core: 2. Of those that a mesh axis runs over, the one named last changes fastest.
Arguments:
- psi_sectors: bfloat16 [32, 8192, 256], P('sector', 'row'), may hold values from -1.5 to 1.5
- stiff_blocks: bfloat16 [64, 5, 128, 128], P('row'), as said below
- mass_blocks: bfloat16 [64, 5, 128, 128], P('row'), as said below
- harmonic_table: int32 [16], replicated, may hold values from 0 to 15, each once
Outputs:
- reduced_stiffness: float32 [16, 512, 512], P('sector', 'row')
- reduced_mass: float32 [16, 512, 512], P('sector', 'row')
Inputs may be any that keep to these rules, and one draw needn't show every extreme that they name: The stiffness is symmetric: stiff_blocks[i, 2 + d] is the transpose of stiff_blocks[i + d, 2 - d], and blocks whose column lies outside 0 to 63 are zero. `mass_blocks`: the mass is symmetric in the same way, and diagonally dominant with a positive diagonal, hence positive definite.
All inputs are finite; a program needn't handle non-finite values.
Results may differ from a plain program's by a relative error of at most 0.0049.
Values may be sent and summed in bfloat16 or wider, within the bound.
A program may use at most 128 MiB of HBM per device.

v0:
```python
import math

import jax
import jax.numpy as jnp
from jax import lax
from jax.sharding import PartitionSpec as P

B = 128
REACH = 2


def padded(block, sides, width):
    for axis, dim in sides:
        count = lax.axis_size(axis)
        forward = [(i, i + 1) for i in range(count - 1)]
        backward = [(target, source) for source, target in forward]
        low = lax.ppermute(
            lax.slice_in_dim(block, block.shape[dim] - width, None, axis=dim), axis, forward
        )
        high = lax.ppermute(lax.slice_in_dim(block, 0, width, axis=dim), axis, backward)
        block = jnp.concatenate([low, block, high], axis=dim)
    return block


def coefficients(harmonic_table, sectors_all):
    sector_ids = jnp.arange(sectors_all, dtype=jnp.int32)
    half_count = sectors_all // 2
    second_freq = jnp.where(harmonic_table == 0, half_count, harmonic_table)
    first_phase = harmonic_table[:, None] * sector_ids[None, :] % sectors_all
    second_phase = second_freq[:, None] * sector_ids[None, :] % sectors_all
    angle_unit = 2.0 * math.pi / sectors_all
    first_angle = first_phase.astype(jnp.float32) * angle_unit
    second_angle = second_phase.astype(jnp.float32) * angle_unit
    zero_pair = (harmonic_table == 0)[:, None]
    low_scale = math.sqrt(1.0 / sectors_all)
    high_scale = math.sqrt(2.0 / sectors_all)
    first_row = jnp.where(zero_pair, low_scale, high_scale) * jnp.cos(first_angle)
    second = jnp.where(
        zero_pair, low_scale * jnp.cos(second_angle), high_scale * jnp.sin(second_angle)
    )
    return jnp.stack([first_row, second], axis=1).reshape(2 * harmonic_table.shape[0], sectors_all)


def per_device(psi_sectors, stiff_blocks, mass_blocks, harmonic_table):
    sec_dev, rows_dev, mode_count = psi_sectors.shape
    sectors_all = sec_dev * lax.axis_size("sector")
    dft_table = coefficients(harmonic_table, sectors_all)
    margin = REACH * B
    combined = jnp.einsum(
        "cs,srm->crm",
        dft_table,
        lax.all_to_all(psi_sectors, "sector", split_axis=1, concat_axis=0, tiled=True).astype(
            jnp.float32
        ),
        precision=lax.Precision.HIGHEST,
    )
    harmonics = lax.all_to_all(
        combined.astype(jnp.bfloat16), "sector", split_axis=0, concat_axis=1, tiled=True
    )
    extended = padded(harmonics, (("row", 1),), margin)
    block_rows = rows_dev // B
    blocks_ext = extended.reshape(sec_dev, block_rows + 2 * REACH, B, mode_count)
    gathered = jnp.stack(
        [blocks_ext[:, offset : offset + block_rows] for offset in range(2 * REACH + 1)], axis=2
    )
    slot_dev = sec_dev // 2

    def paired(field_data):
        split = field_data.reshape(slot_dev, 2, rows_dev, mode_count)
        return split.transpose(0, 2, 1, 3).reshape(slot_dev, rows_dev, 2 * mode_count)

    def project_band(blocks):
        images = jnp.einsum(
            "ijab,cijbm->ciam", blocks, gathered, preferred_element_type=jnp.float32
        )
        return paired(images.astype(jnp.bfloat16).reshape(sec_dev, rows_dev, mode_count))

    left_basis = paired(harmonics)
    stiff_terms = jnp.einsum(
        "sra,srb->sab", left_basis, project_band(stiff_blocks), preferred_element_type=jnp.float32
    )
    mass_terms = jnp.einsum(
        "sra,srb->sab", left_basis, project_band(mass_blocks), preferred_element_type=jnp.float32
    )
    reduced_stiffness, reduced_mass = (
        lax.psum_scatter(stiff_terms, "row", scatter_dimension=1, tiled=True),
        lax.psum_scatter(mass_terms, "row", scatter_dimension=1, tiled=True),
    )
    return (reduced_stiffness, reduced_mass)


def solution(mesh):
    placed = (P("sector", "row", None), P("row", None, None, None), P("row", None, None, None), P())
    return jax.shard_map(
        per_device,
        mesh=mesh,
        in_specs=placed,
        out_specs=(P("sector", "row", None), P("sector", "row", None)),
        check_vma=False,
    )
```

profile of v0, /device:TPU:24, one launch (start us, length us, event | category | flops | bytes accessed | tf_op | source)
XLA Modules:
  0.0 312.1 jit_solution(2027125193981641198)
XLA Ops:
  7.2 0.0 copy-start
  7.2 7.8 %copy.85 = bf16[4,2048,256]{2,0,1:T(4,128)(2,1)} copy(bf16[4,2048,256]{2,1,0:T(8,128)(2,1)} %param.4) | data formatting | bytes 8388608 | tf_op args[0]
  15.0 0.0 copy-start.8
  15.0 4.7 %all-to-all-start = ((bf16[4,2048,256]{2,0,1:T(4,128)(2,1)}), bf16[4,2048,256]{2,0,1:T(4,128)(2,1)}, u32[]{:S(2)}, u32[]{:S(2)}) async-start(bf16[4,2048,256]{2,0,1:T(4,128)(2,1)} %copy.85), calls=%async_computation | async-start | bytes 8388608 | tf_op jit(solution)/shard_map/all_to_all | solution.py:52
  19.7 0.0 reduce-scatter.3.cloned.1.call-start
  19.7 0.0 copy-done.8
  19.8 0.1 fusion.13
  19.9 48.8 %all-to-all-done = bf16[4,2048,256]{2,0,1:T(4,128)(2,1)} async-done(((bf16[4,2048,256]{2,0,1:T(4,128)(2,1)}), bf16[4,2048,256]{2,0,1:T(4,128)(2,1)}, u32[]{:S(2)}, u32[]{:S(2)}) %all-to-all-start) | async-done | bytes 4194336 | tf_op jit(solution)/shard_map/all_to_all | solution.py:52
  68.8 6.6 %copy.129 = bf16[4,8,256,256]{3,0,1,2:T(4,128)(2,1)} copy(bf16[4,8,256,256]{3,0,2,1:T(4,128)(2,1)} %bitcast.2) | data formatting | bytes 8388608 | tf_op jit(solution)/shard_map/all_to_all | solution.py:52
  75.3 6.9 %all_to_all.29 = bf16[32,256,256]{2,0,1:T(8,128)(2,1)} reshape(bf16[8,4,256,256]{3,1,0,2:T(4,128)(2,1)} %bitcast.82) | data formatting | bytes 8388608 | tf_op jit(solution)/shard_map/all_to_all | solution.py:52
  82.3 5.6 %convolution_convert_fusion = bf16[32,256,256]{2,0,1:T(8,128)(2,1)S(1)} fusion(f32[32,32,1]{1,0,2:T(8,128)S(1)} %bitcast.90, bf16[32,256,256]{2,0,1:T(8,128)(2,1)} %all_to_all.29), kind=kOutput, calls=%fused_computation.16 | convolution fusion | flops 807403520 | bytes 8392704 | tf_op jit(solution)/shard_map/cs,srm->crm/dot_general | solution.py:49
  87.8 2.4 copy.87
  90.3 51.5 %all_to_all.36 = bf16[32,256,256]{2,1,0:T(8,128)(2,1)S(1)} all-to-all(bf16[32,256,256]{2,1,0:T(8,128)(2,1)S(1)} %copy.87), channel_id=1, replica_groups=mesh['sector'=8,'row'=4] {'sector'}, dimensions={0} | all-to-all | bytes 8388608 | tf_op jit(solution)/shard_map/all_to_all | solution.py:57
  141.8 0.4 copy.88
  142.2 0.0 copy-start.2
  142.2 2.0 copy-done.2
  144.2 1.0 fusion.24
  145.2 1.3 collective-permute-start
  146.5 5.4 %collective-permute-start.1 = (bf16[4,256,256]{2,1,0:T(8,128)(2,1)}, bf16[4,256,256]{2,1,0:T(8,128)(2,1)}, u32[]{:S(2)}, u32[]{:S(2)}) collective-permute-start(bf16[4,256,256]{2,1,0:T(8,128)(2,1)} %get-tuple-element.8), channel_id=1, source_target_pairs={{1,0},{2,1},{3,2},{5,4},{6,5},{7,6},{9,8},{10,9},{11,10},{13,12},{... | collective-permute-start | bytes 1572872 | tf_op jit(solution)/shard_map/ppermute | solution.py:20
  151.9 6.3 %copy.89 = bf16[2,2048,2,256]{1,3,2,0:T(8,128)(2,1)} copy(bf16[2,2048,2,256]{3,1,2,0:T(8,128)(2,1)} %bitcast.80) | data formatting | bytes 8388608 | tf_op jit(solution)/shard_map/transpose | solution.py:70
  158.2 2.3 collective-permute-done
  160.4 1.3 collective-permute-done.1
  161.7 4.5 %pad_maximum_fusion = bf16[4,2560,256]{2,1,0:T(8,128)(2,1)S(1)} fusion(bf16[4,256,256]{2,1,0:T(8,128)(2,1)} %collective-permute-done.1, bf16[4,2048,256]{2,1,0:T(8,128)(2,1)} %bitcast.81, bf16[4,256,256]{2,1,0:T(8,128)(2,1)S(1)} %collective-permute-done), kind=kLoop, calls=%fused_computation.2 | loop fusion | flops 15728640 | bytes 10485760 | tf_op jit(solution)/shard_map/concatenate | solution.py:21
  166.2 7.3 %fusion.23 = (bf16[4,16,128,256]{3,2,1,0:T(8,128)(2,1)}, bf16[4,16,128,256]{3,2,1,0:T(8,128)(2,1)}, bf16[4,16,128,256]{3,2,1,0:T(8,128)(2,1)}, bf16[4,16,128,256]{3,2,1,0:T(8,128)(2,1)}, bf16[4,16,128,256]{3,2,1,0:T(8,128)(2,1)}) fusion(bf16[4,20,128,256]{3,2,1,0:T(8,128)(2,1)S(1)} %bitcast.78), kind=kLoop, calls=%fused_computation.44 | loop fusion | bytes 41943040 | tf_op jit(solution)/shard_map/slice | solution.py:64
  173.5 0.0 copy-start.6
  173.5 5.0 %fusion.6 = bf16[4,16,5,128,256]{4,3,2,0,1:T(8,128)(2,1)} fusion(bf16[4,16,128,256]{3,2,1,0:T(8,128)(2,1)} %get-tuple-element.6), kind=kLoop, calls=%fused_computation.14 | loop fusion | bytes 8388608
  178.5 0.0 copy-done.6
  178.5 0.0 copy-start.5
  178.5 2.4 fusion.5
  180.9 1.3 copy-done.5
  182.2 0.0 copy-start.4
  182.2 2.4 fusion.4
  184.6 1.3 copy-done.4
  185.9 0.0 copy-start.3
  185.9 2.4 fusion.3
  188.3 1.3 copy-done.3
  189.6 2.3 fusion.2
  191.9 0.0 copy-done
  191.9 8.8 %fusion = bf16[4,16,128,256]{3,2,0,1:T(8,128)(2,1)S(1)} fusion(bf16[4,16,5,128,256]{4,3,2,0,1:T(8,128)(2,1)} %fusion.2, bf16[16,5,128,128]{3,2,1,0:T(8,128)(2,1)S(1)} %copy-done), kind=kOutput, calls=%fused_computation.3 | convolution fusion | flops 2686451712 | bytes 27787264 | tf_op jit(solution)/shard_map/ijab,cijbm->ciam/dot_general | solution.py:73
  200.7 2.2 copy.96
  202.9 6.3 %copy.97 = bf16[2,2048,2,256]{1,3,2,0:T(8,128)(2,1)} copy(bf16[2,2048,2,256]{3,1,2,0:T(8,128)(2,1)} %bitcast.84) | data formatting | bytes 8388608 | tf_op jit(solution)/shard_map/transpose | solution.py:70
  209.2 0.0 copy-start.7
  209.2 7.3 %fusion.25 = f32[2,512,512]{2,1,0:T(8,128)} fusion(bf16[2,2048,512]{1,2,0:T(8,128)(2,1)} %bitcast.86, bf16[2,2048,512]{1,2,0:T(8,128)(2,1)} %bitcast.89), kind=kOutput, calls=%fused_computation.46 | convolution fusion | flops 2147483648 | bytes 10485760 | tf_op jit(solution)/shard_map/sra,srb->sab/dot_general | solution.py:79
  216.5 0.0 reduce-scatter.3.cloned.1.call-update
  216.6 0.3 reduce-scatter.5.cloned.1.call-start
  216.8 0.0 copy-done.7
  216.8 8.8 %fusion.1 = bf16[4,16,128,256]{3,2,0,1:T(8,128)(2,1)S(1)} fusion(bf16[4,16,5,128,256]{4,3,2,0,1:T(8,128)(2,1)} %fusion.2, bf16[16,5,128,128]{3,2,1,0:T(8,128)(2,1)S(1)} %copy-done.7), kind=kOutput, calls=%fused_computation.4 | convolution fusion | flops 2686451712 | bytes 27787264 | tf_op jit(solution)/shard_map/ijab,cijbm->ciam/dot_general | solution.py:73
  225.7 2.3 copy.99
  227.9 6.3 %copy.100 = bf16[2,2048,2,256]{1,3,2,0:T(8,128)(2,1)} copy(bf16[2,2048,2,256]{3,1,2,0:T(8,128)(2,1)} %bitcast.85) | data formatting | bytes 8388608 | tf_op jit(solution)/shard_map/transpose | solution.py:70
  234.2 0.0 copy-start.1
  234.2 7.3 %fusion.26 = f32[2,512,512]{2,1,0:T(8,128)} fusion(bf16[2,2048,512]{1,2,0:T(8,128)(2,1)} %bitcast.87, bf16[2,2048,512]{1,2,0:T(8,128)(2,1)} %bitcast.88), kind=kOutput, calls=%fused_computation.47 | convolution fusion | flops 2147483648 | bytes 10485760 | tf_op jit(solution)/shard_map/sra,srb->sab/dot_general | solution.py:82
  241.6 0.0 reduce-scatter.5.cloned.1.call-update
  241.6 17.9 %reduce-scatter.3.cloned.1.call-done = f32[2,128,512]{2,1,0:T(8,128)} async-done(((f32[2,512,512]{2,1,0:T(8,128)}), f32[2,128,512]{2,1,0:T(8,128)}) %reduce-scatter.3.cloned.1.call-update) | async-done | bytes 524304 | tf_op jit(solution)/shard_map/reduce_scatter | solution.py:86
  259.5 45.7 %reduce-scatter.5.cloned.1.call-done = f32[2,128,512]{2,1,0:T(8,128)} async-done(((f32[2,512,512]{2,1,0:T(8,128)}), f32[2,128,512]{2,1,0:T(8,128)}) %reduce-scatter.5.cloned.1.call-update) | async-done | bytes 524304 | tf_op jit(solution)/shard_map/reduce_scatter | solution.py:87
  305.2 0.0 copy-done.1
  (5 shorter events, 0.0 us)
Async XLA Ops:
  7.2 184.8 %copy-start = (bf16[16,5,128,128]{3,2,1,0:T(8,128)(2,1)S(1)}, bf16[16,5,128,128]{3,2,1,0:T(8,128)(2,1)}, u32[]{:S(2)}) copy-start(bf16[16,5,128,128]{3,2,1,0:T(8,128)(2,1)} %param.5) | copy-start | bytes 7864324
  15.0 4.7 %copy-start.8 = (s32[16]{0:T(128)S(1)}, s32[16]{0:T(128)}, u32[]{:S(2)}) copy-start(s32[16]{0:T(128)} %param.7) | copy-start | bytes 196
  15.0 53.8 %all-to-all-start = ((bf16[4,2048,256]{2,0,1:T(4,128)(2,1)}), bf16[4,2048,256]{2,0,1:T(4,128)(2,1)}, u32[]{:S(2)}, u32[]{:S(2)}) async-start(bf16[4,2048,256]{2,0,1:T(4,128)(2,1)} %copy.85), calls=%async_computation | async-start | bytes 8388608 | tf_op jit(solution)/shard_map/all_to_all | solution.py:52
  19.7 239.9 %reduce-scatter.3.cloned.1.call-start = ((), (), s32[]{:S(2)}) async-start(), calls=%async_computation.4 | async-start | bytes 2621440 | tf_op jit(solution)/shard_map/reduce_scatter | solution.py:86
  142.2 2.0 copy-start.2
  145.2 15.2 %collective-permute-start = (bf16[4,256,256]{2,1,0:T(8,128)(2,1)}, bf16[4,256,256]{2,1,0:T(8,128)(2,1)S(1)}, u32[]{:S(2)}, u32[]{:S(2)}) collective-permute-start(bf16[4,256,256]{2,1,0:T(8,128)(2,1)} %get-tuple-element.7), channel_id=1, source_target_pairs={{0,1},{1,2},{2,3},{4,5},{5,6},{6,7},{8,9},{9,10},{10,11},{12,13},{... | collective-permute-start | bytes 1572872 | tf_op jit(solution)/shard_map/ppermute | solution.py:17
  146.5 15.2 %collective-permute-start.1 = (bf16[4,256,256]{2,1,0:T(8,128)(2,1)}, bf16[4,256,256]{2,1,0:T(8,128)(2,1)}, u32[]{:S(2)}, u32[]{:S(2)}) collective-permute-start(bf16[4,256,256]{2,1,0:T(8,128)(2,1)} %get-tuple-element.8), channel_id=1, source_target_pairs={{1,0},{2,1},{3,2},{5,4},{6,5},{7,6},{9,8},{10,9},{11,10},{13,12},{... | collective-permute-start | bytes 1572872 | tf_op jit(solution)/shard_map/ppermute | solution.py:20
  173.5 5.0 %copy-start.6 = (bf16[4,16,128,256]{3,2,1,0:T(8,128)(2,1)S(1)}, bf16[4,16,128,256]{3,2,1,0:T(8,128)(2,1)}, u32[]{:S(2)}) copy-start(bf16[4,16,128,256]{3,2,1,0:T(8,128)(2,1)} %get-tuple-element.5) | copy-start | bytes 12582916
  178.5 3.7 %copy-start.5 = (bf16[4,16,128,256]{3,2,1,0:T(8,128)(2,1)S(1)}, bf16[4,16,128,256]{3,2,1,0:T(8,128)(2,1)}, u32[]{:S(2)}) copy-start(bf16[4,16,128,256]{3,2,1,0:T(8,128)(2,1)} %get-tuple-element.4) | copy-start | bytes 12582916
  182.2 3.7 %copy-start.4 = (bf16[4,16,128,256]{3,2,1,0:T(8,128)(2,1)S(1)}, bf16[4,16,128,256]{3,2,1,0:T(8,128)(2,1)}, u32[]{:S(2)}) copy-start(bf16[4,16,128,256]{3,2,1,0:T(8,128)(2,1)} %get-tuple-element.3) | copy-start | bytes 12582916
  185.9 3.7 %copy-start.3 = (bf16[4,16,128,256]{3,2,1,0:T(8,128)(2,1)S(1)}, bf16[4,16,128,256]{3,2,1,0:T(8,128)(2,1)}, u32[]{:S(2)}) copy-start(bf16[4,16,128,256]{3,2,1,0:T(8,128)(2,1)} %get-tuple-element.2) | copy-start | bytes 12582916
  209.2 7.6 %copy-start.7 = (bf16[16,5,128,128]{3,2,1,0:T(8,128)(2,1)S(1)}, bf16[16,5,128,128]{3,2,1,0:T(8,128)(2,1)}, u32[]{:S(2)}) copy-start(bf16[16,5,128,128]{3,2,1,0:T(8,128)(2,1)} %param.6) | copy-start | bytes 7864324
  216.6 88.7 %reduce-scatter.5.cloned.1.call-start = ((), (), s32[]{:S(2)}) async-start(), calls=%async_computation.5 | async-start | bytes 2621440 | tf_op jit(solution)/shard_map/reduce_scatter | solution.py:87
  234.2 71.0 %copy-start.1 = (bf16[16,5,128,128]{3,2,1,0:T(8,128)(2,1)S(1)}, bf16[16,5,128,128]{3,2,1,0:T(8,128)(2,1)}, u32[]{:S(2)}) copy-start(bf16[16,5,128,128]{3,2,1,0:T(8,128)(2,1)} %param.5) | copy-start | bytes 7864324
Sparse Core Ops, SparseCore 0:
  216.7 42.7 reduce-scatter.2
  262.4 42.8 reduce-scatter.4
where the time goes:
time: 316 us; the launch traced here: 312 us
  waiting for transfers between devices  116 us (37%)
  local copies, waits for them, and re-layouts  76.2 us (24%)
  blocking collectives  51.5 us (16%)
  matrix products  37.9 us (12%)
  between operations  14.2 us (4%)
  starting transfers between devices  11.6 us (4%)
  other arithmetic  4.65 us (1%)
    all_to_all x1, blocking collectives, per_device(): lax.all_to_all(combined.astype(jnp.bfloat16), 'sector', split_axis=0, con...  51.5 us
    all_to_all x1, waiting for transfers between devices, per_device(): lax.all_to_all(psi_sectors, 'sector', split_axis=1, concat_axis=0, tiled=...  48.8 us
    reduce_scatter x1, waiting for transfers between devices, per_device(): lax.psum_scatter(mass_terms, 'row', scatter_dimension=1, tiled=True)  45.7 us
    unnamed x23, local copies, waits for them, and re-layouts  25.9 us
    transpose x3, local copies, waits for them, and re-layouts, paired(): split.transpose(0, 2, 1, 3).reshape(slot_dev, rows_dev, 2 * mode_count)  18.9 us
    reduce_scatter x1, waiting for transfers between devices, per_device(): lax.psum_scatter(stiff_terms, 'row', scatter_dimension=1, tiled=True)  17.9 us
    dot_general x2, matrix products, project_band(): jnp.einsum('ijab,cijbm->ciam', blocks, gathered, preferred_element_type=j...  17.6 us
    all_to_all x2, local copies, waits for them, and re-layouts, per_device(): lax.all_to_all(psi_sectors, 'sector', split_axis=1, concat_axis=0, tiled=...  13.5 us
  transfers between devices with their start and end apart: 5, of which 5 were waited for; matrix products, arithmetic and copies ran while one was open for 10% of the time, Pallas kernels for 0%

commit v1 on v0

v1 whole, which is shorter than its diff:
```python
import functools
import math

import jax
import jax.numpy as jnp
from jax import lax
from jax.experimental import pallas as pl
from jax.experimental.pallas import tpu as pltpu
from jax.sharding import PartitionSpec as P

MESH = pl.DeviceIdType.MESH
LANES = 128
PACK = 16
CHUNKS = 4


def coefficients(harmonic_table, sectors_all):
    sector_ids = jnp.arange(sectors_all, dtype=jnp.int32)
    half_count = sectors_all // 2
    second_freq = jnp.where(harmonic_table == 0, half_count, harmonic_table)
    first_phase = harmonic_table[:, None] * sector_ids[None, :] % sectors_all
    second_phase = second_freq[:, None] * sector_ids[None, :] % sectors_all
    angle_unit = 2.0 * math.pi / sectors_all
    first_angle = first_phase.astype(jnp.float32) * angle_unit
    second_angle = second_phase.astype(jnp.float32) * angle_unit
    zero_pair = (harmonic_table == 0)[:, None]
    low_scale = math.sqrt(1.0 / sectors_all)
    high_scale = math.sqrt(2.0 / sectors_all)
    first_row = jnp.where(zero_pair, low_scale, high_scale) * jnp.cos(first_angle)
    second = jnp.where(
        zero_pair, low_scale * jnp.cos(second_angle), high_scale * jnp.sin(second_angle)
    )
    return jnp.stack([first_row, second], axis=1)


def flipped(index, step, count):
    total, bit = 0, 1
    while bit < count:
        total = total + bit * lax.rem(lax.div(index, bit) + (step // bit) % 2, 2)
        bit *= 2
    return total


def kernel(cfg, table_ref, psi_ref, stiff_ref, mass_ref, out_k, out_m,
           x_buf, h_buf, p_buf, pt_buf, y_buf, band, g_f32, g_send, g_recv, weights,
           s1, r1, l1, s2, r2, l2, sh, rh, s3, r3, lb):
    n, zn, sec, rows, modes, nblk, nband, blk = cfg
    slots = sec // 2
    part = rows // n
    chunk = part // CHUNKS
    halo = (nband // 2) * blk
    total = 2 * modes
    own_rows = total // zn
    d = lax.axis_index("sector")
    z = lax.axis_index("row")
    order = [j for j in (2, 4, 6, 3, 5, 7) if j < n] + [1]
    order += [j for j in range(1, n) if j not in order]

    barrier = pltpu.get_barrier_semaphore()
    for j in order:
        pl.semaphore_signal(barrier, inc=1, device_id={"sector": flipped(d, j, n)}, device_id_type=MESH)
    for j in range(1, zn):
        pl.semaphore_signal(barrier, inc=1, device_id={"row": lax.rem(z + j, zn)}, device_id_type=MESH)
    pl.semaphore_wait(barrier, n - 1 + zn - 1)

    def first(q, j):
        target = flipped(d, j, n)
        return pltpu.make_async_remote_copy(
            src_ref=psi_ref.at[:, pl.ds(target * part + q * chunk, chunk), :],
            dst_ref=x_buf.at[q, pl.ds(d * sec, sec)],
            send_sem=s1.at[q, j], recv_sem=r1.at[q, j],
            device_id={"sector": target}, device_id_type=MESH)

    def first_own(q):
        return pltpu.make_async_copy(
            psi_ref.at[:, pl.ds(d * part + q * chunk, chunk), :],
            x_buf.at[q, pl.ds(d * sec, sec)], l1.at[q])

    def second(q, h, j):
        target = flipped(d, j, n)
        return pltpu.make_async_remote_copy(
            src_ref=h_buf.at[q, h, pl.ds(target * 2, 2)],
            dst_ref=p_buf.at[h, :, pl.ds(halo + d * part + q * chunk, chunk), :],
            send_sem=s2.at[q, h, j], recv_sem=r2.at[q, h, j],
            device_id={"sector": target}, device_id_type=MESH)

    def second_own(q, h):
        return pltpu.make_async_copy(
            h_buf.at[q, h, pl.ds(d * 2, 2)],
            p_buf.at[h, :, pl.ds(halo + d * part + q * chunk, chunk), :], l2.at[q, h])

    def edge(h, up):
        source = rows if up else halo
        dest = 0 if up else halo + rows
        target = lax.rem(z + (1 if up else zn - 1), zn)
        return pltpu.make_async_remote_copy(
            src_ref=p_buf.at[h, :, pl.ds(source, halo), :],
            dst_ref=p_buf.at[h, :, pl.ds(dest, halo), :],
            send_sem=sh.at[h, int(up)], recv_sem=rh.at[h, int(up)],
            device_id={"row": target}, device_id_type=MESH)

    def third(h, j):
        target = lax.rem(z + j, zn)
        return pltpu.make_async_remote_copy(
            src_ref=g_send.at[h, pl.ds(target * own_rows, own_rows), :],
            dst_ref=g_recv.at[h, j - 1],
            send_sem=s3.at[h, j], recv_sem=r3.at[h, j],
            device_id={"row": target}, device_id_type=MESH)

    @pl.loop(0, CHUNKS)
    def _(q):
        for j in order:
            first(q, j).start()
        first_own(q).start()

    band_copies = [pltpu.make_async_copy(stiff_ref, band.at[0], lb.at[0]),
                   pltpu.make_async_copy(mass_ref, band.at[1], lb.at[1])]
    for copy in band_copies:
        copy.start()

    @pl.when(z == 0)
    def _():
        for h in range(slots):
            p_buf[h, :, pl.ds(0, halo), :] = jnp.zeros((2, halo, modes), p_buf.dtype)

    @pl.when(z == zn - 1)
    def _():
        for h in range(slots):
            p_buf[h, :, pl.ds(halo + rows, halo), :] = jnp.zeros((2, halo, modes), p_buf.dtype)

    wide_rows, wide_cols = 2 * n * PACK, n * sec * PACK
    spread_rows = (lax.broadcasted_iota(jnp.int32, (wide_rows, LANES), 0) >> 4
                   == lax.broadcasted_iota(jnp.int32, (wide_rows, LANES), 1)).astype(jnp.float32).astype(jnp.bfloat16)
    spread_cols = (lax.broadcasted_iota(jnp.int32, (LANES, wide_cols), 1) >> 4
                   == lax.broadcasted_iota(jnp.int32, (LANES, wide_cols), 0)).astype(jnp.float32).astype(jnp.bfloat16)
    same = ((lax.broadcasted_iota(jnp.int32, (wide_rows, wide_cols), 0) & (PACK - 1))
            == (lax.broadcasted_iota(jnp.int32, (wide_rows, wide_cols), 1) & (PACK - 1)))
    for h in range(slots):
        value = table_ref[h]
        high = value.astype(jnp.bfloat16)
        low = (value - high.astype(jnp.float32)).astype(jnp.bfloat16)
        for index, piece in enumerate((high, low)):
            tall = jnp.dot(spread_rows, piece, preferred_element_type=jnp.float32).astype(jnp.bfloat16)
            full = jnp.dot(tall, spread_cols, preferred_element_type=jnp.float32)
            weights[h, index] = jnp.where(same, full, 0.0).astype(jnp.bfloat16)

    @pl.loop(0, CHUNKS)
    def _(q):
        for j in order:
            first(q, j).wait_recv()
        first_own(q).wait()

        @pl.loop(0, chunk // PACK)
        def _(g):
            at = pl.ds(pl.multiple_of(g * PACK, PACK), PACK)
            x = x_buf[q, :, at, :].reshape(wide_cols, modes)
            for h in range(slots):
                value = (jnp.dot(weights[h, 0], x, preferred_element_type=jnp.float32)
                         + jnp.dot(weights[h, 1], x, preferred_element_type=jnp.float32))
                h_buf[q, h, :, at, :] = value.astype(jnp.bfloat16).reshape(2 * n, PACK, modes)

        for j in order:
            second(q, 0, j).start()
        second_own(q, 0).start()

    for h in range(1, slots):
        @pl.loop(0, CHUNKS)
        def _(q):
            for j in order:
                second(q, h, j).start()
            second_own(q, h).start()

    for copy in band_copies:
        copy.wait()

    def block_row(h, i):
        at = pl.ds(pl.multiple_of(i * blk, blk), blk)
        blocks = jnp.concatenate(
            [jnp.concatenate([band[which, i, k] for k in range(nband)], axis=1) for which in range(2)], axis=0)
        window = pl.ds(pl.multiple_of(i * blk, blk), nband * blk)
        inner = pl.ds(pl.multiple_of(i * blk + halo, blk), blk)
        for k in range(2):
            image = jnp.dot(blocks, p_buf[h, k, window, :], preferred_element_type=jnp.float32).astype(jnp.bfloat16)
            y_buf[at, k * modes:(k + 1) * modes] = image[:blk]
            y_buf[at, total + k * modes:total + (k + 1) * modes] = image[blk:]
            pt_buf[k * modes:(k + 1) * modes, at] = p_buf[h, k, inner, :].T

    reach = nband // 2

    @pl.loop(0, slots)
    def _(h):
        @pl.loop(0, CHUNKS)
        def _(q):
            for j in order:
                second(q, h, j).wait_recv()
            second_own(q, h).wait()

        @pl.when(z < zn - 1)
        def _():
            edge(h, True).start()

        @pl.when(z > 0)
        def _():
            edge(h, False).start()

        @pl.loop(reach, nblk - reach)
        def _(i):
            block_row(h, i)

        @pl.when(z > 0)
        def _():
            edge(h, True).wait_recv()

        @pl.when(z < zn - 1)
        def _():
            edge(h, False).wait_recv()

        @pl.loop(0, 2 * reach)
        def _(i):
            block_row(h, lax.rem(i + nblk - reach, nblk))

        @pl.loop(0, 2)
        def _(k):
            at = pl.ds(pl.multiple_of(k * modes, modes), modes)
            for c in range(2 * total // modes):
                value = jnp.dot(pt_buf[at, :], y_buf[:, c * modes:(c + 1) * modes],
                                preferred_element_type=jnp.float32)
                g_f32[at, c * modes:(c + 1) * modes] = value
                g_send[h, at, c * modes:(c + 1) * modes] = value.astype(jnp.bfloat16)

        for j in range(1, zn):
            third(h, j).start()
        mine = pl.ds(pl.multiple_of(z * own_rows, own_rows), own_rows)
        out_k[h] = g_f32[mine, :total]
        out_m[h] = g_f32[mine, total:]

    @pl.loop(0, slots)
    def _(h):
        for j in range(1, zn):
            third(h, j).wait_recv()
        for out, start in ((out_k, 0), (out_m, total)):
            value = out[h]
            for j in range(1, zn):
                value = value + g_recv[h, j - 1, :, start:start + total].astype(jnp.float32)
            out[h] = value

    @pl.loop(0, CHUNKS)
    def _(q):
        for j in order:
            first(q, j).wait_send()
            for h in range(slots):
                second(q, h, j).wait_send()

    @pl.loop(0, slots)
    def _(h):
        for j in range(1, zn):
            third(h, j).wait_send()

        @pl.when(z < zn - 1)
        def _():
            edge(h, True).wait_send()

        @pl.when(z > 0)
        def _():
            edge(h, False).wait_send()


def per_device(psi_sectors, stiff_blocks, mass_blocks, harmonic_table):
    sec, rows, modes = psi_sectors.shape
    nblk, nband, blk, _ = stiff_blocks.shape
    n, zn = lax.axis_size("sector"), lax.axis_size("row")
    sectors_all = sec * n
    slots = sec // 2
    table = coefficients(harmonic_table, sectors_all).reshape(n, slots, 2, sectors_all)
    table = table.transpose(1, 0, 2, 3).reshape(slots, 2 * n, sectors_all)
    table = jnp.pad(table, ((0, 0), (0, LANES - 2 * n), (0, LANES - sectors_all)))
    part = rows // n
    chunk = part // CHUNKS
    halo = (nband // 2) * blk
    total = 2 * modes
    own_rows = total // zn
    bf16, f32 = jnp.bfloat16, jnp.float32
    dma = pltpu.SemaphoreType.DMA
    vmem = pl.BlockSpec(memory_space=pltpu.VMEM)
    hbm = pl.BlockSpec(memory_space=pl.ANY)
    out = jax.ShapeDtypeStruct((slots, own_rows, total), f32)
    return pl.pallas_call(
        functools.partial(kernel, (n, zn, sec, rows, modes, nblk, nband, blk)),
        out_shape=(out, out),
        in_specs=[vmem, hbm, hbm, hbm],
        out_specs=(vmem, vmem),
        scratch_shapes=[
            pltpu.VMEM((CHUNKS, sectors_all, chunk, modes), bf16),
            pltpu.VMEM((CHUNKS, slots, 2 * n, chunk, modes), bf16),
            pltpu.VMEM((slots, 2, rows + 2 * halo, modes), bf16),
            pltpu.VMEM((total, rows), bf16),
            pltpu.VMEM((rows, 2 * total), bf16),
            pltpu.VMEM((2, nblk, nband, blk, blk), bf16),
            pltpu.VMEM((total, 2 * total), f32),
            pltpu.VMEM((slots, total, 2 * total), bf16),
            pltpu.VMEM((slots, zn - 1, own_rows, 2 * total), bf16),
            pltpu.VMEM((slots, 2, 2 * n * PACK, sectors_all * PACK), bf16),
            dma((CHUNKS, n)), dma((CHUNKS, n)), dma((CHUNKS,)),
            dma((CHUNKS, slots, n)), dma((CHUNKS, slots, n)), dma((CHUNKS, slots)),
            dma((slots, 2)), dma((slots, 2)),
            dma((slots, zn)), dma((slots, zn)),
            dma((2,)),
        ],
        compiler_params=pltpu.CompilerParams(
            collective_id=0, has_side_effects=True, vmem_limit_bytes=60 * 1024 * 1024),
    )(table, psi_sectors, stiff_blocks, mass_blocks)


def solution(mesh):
    placed = (P("sector", "row", None), P("row", None, None, None), P("row", None, None, None), P())
    return jax.shard_map(
        per_device,
        mesh=mesh,
        in_specs=placed,
        out_specs=(P("sector", "row", None), P("sector", "row", None)),
        check_vma=False,
    )
```

time: 316 us -> 155 us (0.49)
  Pallas kernels: 0 us -> 145 us
  waiting for transfers between devices: 116 us -> 0 us
  local copies, waits for them, and re-layouts: 76.2 us -> 5.75 us
  blocking collectives: 51.5 us -> 0 us
  matrix products: 37.9 us -> 0 us
  between operations: 14.2 us -> 0.67 us
  starting transfers between devices: 11.6 us -> 0 us
    pallas_call x0 -> x1, Pallas kernels: none -> 145 us  [per_device(): pl.pallas_call(functools.partial(kernel, (n, zn, sec, rows, modes, nblk,...]
    reduce_scatter x2 -> x0, waiting for transfers between devices: 63.6 us -> none  [the longest x1 45.7 us: per_device(): lax.psum_scatter(mass_terms, 'row', scatter_dimension=1, tiled=True)]
    all_to_all x1 -> x0, blocking collectives: 51.5 us -> none  [per_device(): lax.all_to_all(combined.astype(jnp.bfloat16), 'sector', split_axis=0, con...]
    all_to_all x1 -> x0, waiting for transfers between devices: 48.8 us -> none  [per_device(): lax.all_to_all(psi_sectors, 'sector', split_axis=1, concat_axis=0, tiled=...]
    dot_general x5 -> x0, matrix products: 37.9 us -> none  [the longest x2 17.6 us: project_band(): jnp.einsum('ijab,cijbm->ciam', blocks, gathered, preferred_element_type=j...]
    unnamed x23 -> x2, local copies, waits for them, and re-layouts: 25.9 us -> 3.74 us
    transpose x3 -> x1, local copies, waits for them, and re-layouts: 18.9 us -> 0.01 us  [per_device(): table = table.transpose(1, 0, 2, 3).reshape(slots, 2 * n, sectors_all)]
    all_to_all x3 -> x0, local copies, waits for them, and re-layouts: 13.9 us -> none  [the longest x2 13.5 us: per_device(): lax.all_to_all(psi_sectors, 'sector', split_axis=1, concat_axis=0, tiled=...]
  transfers between devices with their start and end apart: 5 -> 0, of which waited for: 5 -> 0; matrix products, arithmetic and copies ran while one was open for 10% -> 0% of each run, Pallas kernels for 0% -> 0%
where the time goes in v1:
time: 155 us; the launch traced here: 154 us
  Pallas kernels  145 us (94%)
  local copies, waits for them, and re-layouts  5.75 us (4%)
  other arithmetic  2.14 us (1%)
    pallas_call x1, Pallas kernels, per_device(): pl.pallas_call(functools.partial(kernel, (n, zn, sec, rows, modes, nblk,...  145 us
    unnamed x2, local copies, waits for them, and re-layouts  3.74 us

profile of v1, /device:TPU:24, one launch (start us, length us, event | category | flops | bytes accessed | tf_op | source)
XLA Modules:
  0.0 153.8 jit_solution(9777795799382928857)
XLA Ops:
  0.6 0.7 broadcast_select_fusion.1
  1.3 0.7 broadcast_compare_fusion
  1.9 0.1 broadcast_in_dim.29
  2.0 0.1 copy.16
  2.1 0.7 broadcast_select_fusion
  2.8 0.1 mul.122
  2.9 0.1 copy.17
  3.0 0.1 mul.114
  3.0 0.1 copy.14
  3.1 0.7 mul.116
  3.9 0.1 copy.15
  4.0 0.2 fusion.4
  4.1 0.7 pad.4.table_ref
  4.8 145.3 %shard_map.59 = (f32[2,128,512]{2,1,0:T(8,128)}, f32[2,128,512]{2,1,0:T(8,128)}) custom-call(f32[2,128,128]{2,1,0:T(8,128)} %pad.4.table_ref, bf16[4,2048,256]{2,1,0:T(8,128)(2,1)} %psi_ref.1, bf16[16,5,128,128]{3,2,1,0:T(8,128)(2,1)} %stiff_ref.1, bf16[16,5,128,128]{3,2,1,0:T(8,128)(2,1)} %mass_ref.1), custom_call_target="tpu_custom_call" | custom-call | tf_op jit(solution)/shard_map/pallas_call | solution.py:287
  150.1 1.9 %copy.21 = f32[2,128,512]{2,1,0:T(8,128)} copy(f32[2,128,512]{2,1,0:T(8,128)} %get-tuple-element.6) | data formatting | bytes 1048576
  151.9 1.9 %copy.22 = f32[2,128,512]{2,1,0:T(8,128)} copy(f32[2,128,512]{2,1,0:T(8,128)} %get-tuple-element.7) | data formatting | bytes 1048576
  (2 shorter events, 0.0 us)

commit v2 on v1

v2 whole, which is shorter than its diff:
```python
import functools
import math

import jax
import jax.numpy as jnp
from jax import lax
from jax.experimental import pallas as pl
from jax.experimental.pallas import tpu as pltpu
from jax.sharding import PartitionSpec as P

MESH = pl.DeviceIdType.MESH
LANES = 128
PACK = 16
CHUNKS = 4


def flipped(index, step, count):
    total, bit = 0, 1
    while bit < count:
        total = total + bit * lax.rem(lax.div(index, bit) + (step // bit) % 2, 2)
        bit *= 2
    return total


def kernel(cfg, table_ref, psi_ref, stiff_ref, mass_ref, out_k, out_m,
           x_buf, h_buf, p_buf, pt_buf, y_buf, band, g_f32, g_send, g_recv, weights,
           s1, r1, l1, sp, rp, lp, s2, r2, l2, sh, rh, s3, r3, lb):
    n, zn, sec, rows, modes, nblk, nband, blk = cfg
    slots = sec // 2
    part = rows // n
    chunk = part // CHUNKS
    reach = nband // 2
    halo = reach * blk
    total = 2 * modes
    own_rows = total // zn
    halves = modes // LANES
    cols = total // LANES
    groups = slots * cols
    sectors_all = n * sec
    d = lax.axis_index("sector")
    z = lax.axis_index("row")
    order = [j for j in (2, 4, 6, 3, 5, 7) if j < n] + [1]
    order += [j for j in range(1, n) if j not in order]

    barrier = pltpu.get_barrier_semaphore()
    for j in order:
        pl.semaphore_signal(barrier, inc=1, device_id={"sector": flipped(d, j, n)}, device_id_type=MESH)
    for j in range(1, zn):
        pl.semaphore_signal(barrier, inc=1, device_id={"row": lax.rem(z + j, zn)}, device_id_type=MESH)
    pl.semaphore_wait(barrier, n - 1 + zn - 1)

    def first(q, j):
        target = flipped(d, j, n)
        return pltpu.make_async_remote_copy(
            src_ref=psi_ref.at[:, pl.ds(target * part + q * chunk, chunk), :],
            dst_ref=x_buf.at[q, pl.ds(d * sec, sec)],
            send_sem=s1.at[q, j], recv_sem=r1.at[q, j],
            device_id={"sector": target}, device_id_type=MESH)

    def first_own(q):
        return pltpu.make_async_copy(
            psi_ref.at[:, pl.ds(d * part + q * chunk, chunk), :],
            x_buf.at[q, pl.ds(d * sec, sec)], l1.at[q])

    def early(q, j):
        target = flipped(d, j, n)
        return pltpu.make_async_remote_copy(
            src_ref=h_buf.at[pl.ds(0, halves), target, pl.ds(q * chunk, chunk), :],
            dst_ref=p_buf.at[pl.ds(0, halves), pl.ds(halo + d * part + q * chunk, chunk), :],
            send_sem=sp.at[q, j], recv_sem=rp.at[q, j],
            device_id={"sector": target}, device_id_type=MESH)

    def early_own(q):
        return pltpu.make_async_copy(
            h_buf.at[pl.ds(0, halves), d, pl.ds(q * chunk, chunk), :],
            p_buf.at[pl.ds(0, halves), pl.ds(halo + d * part + q * chunk, chunk), :], lp.at[q])

    def second(g, j):
        target = flipped(d, j, n)
        return pltpu.make_async_remote_copy(
            src_ref=h_buf.at[g, target],
            dst_ref=p_buf.at[g, pl.ds(halo + d * part, part), :],
            send_sem=s2.at[g, j], recv_sem=r2.at[g, j],
            device_id={"sector": target}, device_id_type=MESH)

    def second_own(g):
        return pltpu.make_async_copy(
            h_buf.at[g, d], p_buf.at[g, pl.ds(halo + d * part, part), :], l2.at[g])

    def second_start(g):
        for j in order:
            second(g, j).start()
        second_own(g).start()

    def edge(g, up):
        source = rows if up else halo
        dest = 0 if up else halo + rows
        target = lax.rem(z + (1 if up else zn - 1), zn)
        return pltpu.make_async_remote_copy(
            src_ref=p_buf.at[g, pl.ds(source, halo), :],
            dst_ref=p_buf.at[g, pl.ds(dest, halo), :],
            send_sem=sh.at[g, int(up)], recv_sem=rh.at[g, int(up)],
            device_id={"row": target}, device_id_type=MESH)

    def row_group(device):
        return lax.div(device * own_rows, LANES)

    def third(h, j, c, whole):
        target = lax.rem(z + j, zn)
        start, width = (0, (c + 1) * 2 * LANES) if whole else (c * 2 * LANES, 2 * LANES)
        return pltpu.make_async_remote_copy(
            src_ref=g_send.at[h, pl.ds(target * own_rows, own_rows), pl.ds(start, width)],
            dst_ref=g_recv.at[h, j - 1, :, pl.ds(start, width)],
            send_sem=s3.at[h, j, c], recv_sem=r3.at[h, j, c],
            device_id={"row": target}, device_id_type=MESH)

    def third_do(h, c, what):
        for j in range(1, zn):
            held = row_group(z if what == "wait_recv" else lax.rem(z + j, zn))

            @pl.when(held == c)
            def _():
                getattr(third(h, j, c, True), what)()

            @pl.when(held < c)
            def _():
                getattr(third(h, j, c, False), what)()

    @pl.loop(0, CHUNKS)
    def _(q):
        for j in order:
            first(q, j).start()
        first_own(q).start()

    band_copies = [pltpu.make_async_copy(stiff_ref, band.at[0], lb.at[0]),
                   pltpu.make_async_copy(mass_ref, band.at[1], lb.at[1])]
    for copy in band_copies:
        copy.start()

    @pl.when(z == 0)
    def _():
        @pl.loop(0, groups)
        def _(g):
            p_buf[g, pl.ds(0, halo), :] = jnp.zeros((halo, LANES), p_buf.dtype)

    @pl.when(z == zn - 1)
    def _():
        @pl.loop(0, groups)
        def _(g):
            p_buf[g, pl.ds(halo + rows, halo), :] = jnp.zeros((halo, LANES), p_buf.dtype)

    wide_rows, wide_cols = 2 * n * PACK, sectors_all * PACK

    def spread(shape, long):
        return ((lax.broadcasted_iota(jnp.int32, shape, long) >> 4) == lax.broadcasted_iota(
            jnp.int32, shape, 1 - long)).astype(jnp.float32).astype(jnp.bfloat16)

    spread_rows = spread((wide_rows, LANES), 0)
    spread_cols = spread((LANES, wide_cols), 1)
    same = ((lax.broadcasted_iota(jnp.int32, (wide_rows, wide_cols), 0) & (PACK - 1))
            == (lax.broadcasted_iota(jnp.int32, (wide_rows, wide_cols), 1) & (PACK - 1)))
    line = lax.broadcasted_iota(jnp.int32, (LANES, LANES), 0)
    sector = lax.broadcasted_iota(jnp.int32, (LANES, LANES), 1)
    for h in range(slots):
        pair = jnp.zeros((LANES, LANES), jnp.int32)
        for e in range(n):
            pair = jnp.where((line == e) | (line == n + e), table_ref[e * slots + h], pair)
        lone = pair == 0
        upper = line >= n
        turns = jnp.where(lone & upper, sectors_all // 2, pair) * sector
        turns = turns + jnp.where(upper & jnp.logical_not(lone), sectors_all - sectors_all // 4, 0)
        turns = turns & (sectors_all - 1)
        scale = jnp.where(lone, math.sqrt(1.0 / sectors_all), math.sqrt(2.0 / sectors_all))
        value = scale * jnp.cos(turns.astype(jnp.float32) * (2.0 * math.pi / sectors_all))
        high = value.astype(jnp.bfloat16)
        low = (value - high.astype(jnp.float32)).astype(jnp.bfloat16)
        for index, piece in enumerate((high, low)):
            tall = jnp.dot(spread_rows, piece, preferred_element_type=jnp.float32).astype(jnp.bfloat16)
            full = jnp.dot(tall, spread_cols, preferred_element_type=jnp.float32)
            weights[h, index] = jnp.where(same, full, 0.0).astype(jnp.bfloat16)

    @pl.loop(0, CHUNKS)
    def _(q):
        for j in order:
            first(q, j).wait_recv()
        first_own(q).wait()

        @pl.loop(0, chunk // PACK)
        def _(t):
            x = x_buf[q, :, pl.ds(pl.multiple_of(t * PACK, PACK), PACK), :].reshape(wide_cols, modes)
            at = pl.ds(pl.multiple_of(q * chunk + t * PACK, PACK), PACK)
            for h in range(slots):
                value = (jnp.dot(weights[h, 0], x, preferred_element_type=jnp.float32)
                         + jnp.dot(weights[h, 1], x, preferred_element_type=jnp.float32)).astype(jnp.bfloat16)
                for c in range(cols):
                    k, half = c // halves, c % halves
                    h_buf[h * cols + c, :, at, :] = value[
                        k * n * PACK:(k + 1) * n * PACK, half * LANES:(half + 1) * LANES].reshape(n, PACK, LANES)

        for j in order:
            early(q, j).start()
        early_own(q).start()

    second_start(halves)

    for copy in band_copies:
        copy.wait()

    def block_row(g, c, i):
        at = pl.ds(pl.multiple_of(i * blk, blk), blk)
        blocks = jnp.concatenate(
            [jnp.concatenate([band[which, i, k] for k in range(nband)], axis=1) for which in range(2)], axis=0)
        window = p_buf[g, pl.ds(pl.multiple_of(i * blk, blk), nband * blk), :]
        image = jnp.dot(blocks, window, preferred_element_type=jnp.float32).astype(jnp.bfloat16)
        y_buf[at, c * 2 * LANES:c * 2 * LANES + LANES] = image[:blk]
        y_buf[at, c * 2 * LANES + LANES:(c + 1) * 2 * LANES] = image[blk:]
        pt_buf[c * LANES:(c + 1) * LANES, at] = window[halo:halo + blk].T

    def gram(h, first_row, row_count, c):
        span = slice(c * 2 * LANES, (c + 1) * 2 * LANES)
        value = jnp.dot(pt_buf[first_row:first_row + row_count, :], y_buf[:, span],
                        preferred_element_type=jnp.float32)
        g_f32[first_row:first_row + row_count, span] = value
        g_send[h, first_row:first_row + row_count, span] = value.astype(jnp.bfloat16)

    @pl.loop(0, slots)
    def _(h):
        for c in range(cols):
            g = h * cols + c

            def arrived():
                for j in order:
                    second(g, j).wait_recv()
                second_own(g).wait()

            if c == 0:
                @pl.when(h == 0)
                def _():
                    @pl.loop(0, CHUNKS)
                    def _(q):
                        for j in order:
                            early(q, j).wait_recv()
                        early_own(q).wait()

                    second_start(halves + 1)
            if c < halves:
                pl.when(h > 0)(arrived)
            else:
                arrived()

            @pl.when((g >= halves) & (g + 2 < groups))
            def _():
                second_start(g + 2)

            @pl.when(z < zn - 1)
            def _():
                edge(g, True).start()

            @pl.when(z > 0)
            def _():
                edge(g, False).start()

            @pl.loop(reach, nblk - reach)
            def _(i):
                block_row(g, c, i)

            @pl.when(z > 0)
            def _():
                edge(g, True).wait_recv()

            @pl.when(z < zn - 1)
            def _():
                edge(g, False).wait_recv()

            @pl.loop(0, 2 * reach)
            def _(i):
                block_row(g, c, lax.rem(i + nblk - reach, nblk))

            for b in range(c):
                gram(h, c * LANES, LANES, b)
            gram(h, 0, (c + 1) * LANES, c)
            third_do(h, c, "start")

        mine = pl.ds(pl.multiple_of(z * own_rows, own_rows), own_rows)
        for c in range(cols):
            out_k[h, :, c * LANES:(c + 1) * LANES] = g_f32[mine, c * 2 * LANES:c * 2 * LANES + LANES]
            out_m[h, :, c * LANES:(c + 1) * LANES] = g_f32[mine, c * 2 * LANES + LANES:(c + 1) * 2 * LANES]

    @pl.loop(0, slots)
    def _(h):
        for c in range(cols):
            third_do(h, c, "wait_recv")
        for c in range(cols):
            for which, out in enumerate((out_k, out_m)):
                start = (2 * c + which) * LANES
                value = out[h, :, c * LANES:(c + 1) * LANES]
                for j in range(1, zn):
                    value = value + g_recv[h, j - 1, :, start:start + LANES].astype(jnp.float32)
                out[h, :, c * LANES:(c + 1) * LANES] = value

    @pl.loop(0, CHUNKS)
    def _(q):
        for j in order:
            first(q, j).wait_send()
            early(q, j).wait_send()

    @pl.loop(halves, groups)
    def _(g):
        for j in order:
            second(g, j).wait_send()

    @pl.loop(0, groups)
    def _(g):
        @pl.when(z < zn - 1)
        def _():
            edge(g, True).wait_send()

        @pl.when(z > 0)
        def _():
            edge(g, False).wait_send()

    @pl.loop(0, slots)
    def _(h):
        for c in range(cols):
            third_do(h, c, "wait_send")


def per_device(psi_sectors, stiff_blocks, mass_blocks, harmonic_table):
    sec, rows, modes = psi_sectors.shape
    nblk, nband, blk, _ = stiff_blocks.shape
    n, zn = lax.axis_size("sector"), lax.axis_size("row")
    sectors_all = sec * n
    slots = sec // 2
    part = rows // n
    chunk = part // CHUNKS
    halo = (nband // 2) * blk
    total = 2 * modes
    cols = total // LANES
    own_rows = total // zn
    bf16, f32 = jnp.bfloat16, jnp.float32
    dma = pltpu.SemaphoreType.DMA
    vmem = pl.BlockSpec(memory_space=pltpu.VMEM)
    hbm = pl.BlockSpec(memory_space=pl.ANY)
    out = jax.ShapeDtypeStruct((slots, own_rows, total), f32)
    return pl.pallas_call(
        functools.partial(kernel, (n, zn, sec, rows, modes, nblk, nband, blk)),
        out_shape=(out, out),
        in_specs=[pl.BlockSpec(memory_space=pltpu.SMEM), hbm, hbm, hbm],
        out_specs=(vmem, vmem),
        scratch_shapes=[
            pltpu.VMEM((CHUNKS, sectors_all, chunk, modes), bf16),
            pltpu.VMEM((slots * cols, n, part, LANES), bf16),
            pltpu.VMEM((slots * cols, rows + 2 * halo, LANES), bf16),
            pltpu.VMEM((total, rows), bf16),
            pltpu.VMEM((rows, 2 * total), bf16),
            pltpu.VMEM((2, nblk, nband, blk, blk), bf16),
            pltpu.VMEM((total, 2 * total), f32),
            pltpu.VMEM((slots, total, 2 * total), bf16),
            pltpu.VMEM((slots, zn - 1, own_rows, 2 * total), bf16),
            pltpu.VMEM((slots, 2, 2 * n * PACK, sectors_all * PACK), bf16),
            dma((CHUNKS, n)), dma((CHUNKS, n)), dma((CHUNKS,)),
            dma((CHUNKS, n)), dma((CHUNKS, n)), dma((CHUNKS,)),
            dma((slots * cols, n)), dma((slots * cols, n)), dma((slots * cols,)),
            dma((slots * cols, 2)), dma((slots * cols, 2)),
            dma((slots, zn, cols)), dma((slots, zn, cols)),
            dma((2,)),
        ],
        compiler_params=pltpu.CompilerParams(
            collective_id=0, has_side_effects=True, vmem_limit_bytes=60 * 1024 * 1024),
    )(harmonic_table, psi_sectors, stiff_blocks, mass_blocks)


def solution(mesh):
    placed = (P("sector", "row", None), P("row", None, None, None), P("row", None, None, None), P())
    return jax.shard_map(
        per_device,
        mesh=mesh,
        in_specs=placed,
        out_specs=(P("sector", "row", None), P("sector", "row", None)),
        check_vma=False,
    )
```

time: 155 us -> 176 us (1.14)
  Pallas kernels: 145 us -> 172 us
  other arithmetic: 2.14 us -> 0 us
  local copies, waits for them, and re-layouts: 5.75 us -> 3.74 us
    pallas_call x1, Pallas kernels: 145 us -> 172 us  [per_device(): pl.pallas_call(functools.partial(kernel, (n, zn, sec, rows, modes, nblk,...]
where the time goes in v2:
time: 176 us
  Pallas kernels  172 us (98%)
  local copies, waits for them, and re-layouts  3.74 us (2%)
    pallas_call x1, Pallas kernels, per_device(): pl.pallas_call(functools.partial(kernel, (n, zn, sec, rows, modes, nblk,...  172 us
    unnamed x2, local copies, waits for them, and re-layouts  3.74 us

profile of v2, /device:TPU:24, one launch (start us, length us, event | category | flops | bytes accessed | tf_op | source)
XLA Modules:
  0.0 176.0 jit_solution(537487288566064357)
XLA Ops:
  0.6 171.6 %shard_map.59 = (f32[2,128,512]{2,1,0:T(8,128)}, f32[2,128,512]{2,1,0:T(8,128)}) custom-call(s32[16]{0:T(128)} %table_ref.1, bf16[4,2048,256]{2,1,0:T(8,128)(2,1)} %psi_ref.1, bf16[16,5,128,128]{3,2,1,0:T(8,128)(2,1)} %stiff_ref.1, bf16[16,5,128,128]{3,2,1,0:T(8,128)(2,1)} %mass_ref.1), custom_call_target="tpu_custom_call" | custom-call | tf_op jit(solution)/shard_map/pallas_call | solution.py:345
  172.2 1.9 %copy.8 = f32[2,128,512]{2,1,0:T(8,128)} copy(f32[2,128,512]{2,1,0:T(8,128)} %get-tuple-element.4) | data formatting | bytes 1048576
  174.1 1.9 %copy.9 = f32[2,128,512]{2,1,0:T(8,128)} copy(f32[2,128,512]{2,1,0:T(8,128)} %get-tuple-element.5) | data formatting | bytes 1048576

commit v3 on v2

--- a/solution.py
+++ b/solution.py
@@ -36,6 +36,8 @@
     halves = modes // LANES
     cols = total // LANES
     groups = slots * cols
+    place = [(c % 2) * (cols // 2) + c // 2 for c in range(cols)]
+    turn = [place.index(p) for p in range(cols)]
     sectors_all = n * sec
     d = lax.axis_index("sector")
     z = lax.axis_index("row")
@@ -103,13 +105,17 @@
             device_id={"row": target}, device_id_type=MESH)
 
     def row_group(device):
-        return lax.div(device * own_rows, LANES)
+        group = lax.div(device * own_rows, LANES)
+        return lax.rem(group, 2) * (cols // 2) + lax.div(group, 2)
+
+    def row_start(device):
+        return row_group(device) * LANES + lax.rem(device * own_rows, LANES)
 
     def third(h, j, c, whole):
         target = lax.rem(z + j, zn)
         start, width = (0, (c + 1) * 2 * LANES) if whole else (c * 2 * LANES, 2 * LANES)
         return pltpu.make_async_remote_copy(
-            src_ref=g_send.at[h, pl.ds(target * own_rows, own_rows), pl.ds(start, width)],
+            src_ref=g_send.at[h, pl.ds(row_start(target), own_rows), pl.ds(start, width)],
             dst_ref=g_recv.at[h, j - 1, :, pl.ds(start, width)],
             send_sem=s3.at[h, j, c], recv_sem=r3.at[h, j, c],
             device_id={"row": target}, device_id_type=MESH)
@@ -193,7 +199,7 @@
                 value = (jnp.dot(weights[h, 0], x, preferred_element_type=jnp.float32)
                          + jnp.dot(weights[h, 1], x, preferred_element_type=jnp.float32)).astype(jnp.bfloat16)
                 for c in range(cols):
-                    k, half = c // halves, c % halves
+                    k, half = turn[c] // halves, turn[c] % halves
                     h_buf[h * cols + c, :, at, :] = value[
                         k * n * PACK:(k + 1) * n * PACK, half * LANES:(half + 1) * LANES].reshape(n, PACK, LANES)
 
@@ -223,42 +229,43 @@
         g_f32[first_row:first_row + row_count, span] = value
         g_send[h, first_row:first_row + row_count, span] = value.astype(jnp.bfloat16)
 
+    def take(g, c, begin):
+        def arrived():
+            for j in order:
+                second(g, j).wait_recv()
+            second_own(g).wait()
+
+        if begin and c == 0:
+            @pl.loop(0, CHUNKS)
+            def _(q):
+                for j in order:
+                    early(q, j).wait_recv()
+                early_own(q).wait()
+
+            second_start(halves + 1)
+        elif c >= halves:
+            arrived()
+        else:
+            pl.when(g >= halves)(arrived)
+
+        @pl.when((g >= halves) & (g + 2 < groups))
+        def _():
+            second_start(g + 2)
+
+        @pl.when(z < zn - 1)
+        def _():
+            edge(g, True).start()
+
+        @pl.when(z > 0)
+        def _():
+            edge(g, False).start()
+
+    take(0, 0, True)
+
     @pl.loop(0, slots)
     def _(h):
         for c in range(cols):
             g = h * cols + c
-
-            def arrived():
-                for j in order:
-                    second(g, j).wait_recv()
-                second_own(g).wait()
-
-            if c == 0:
-                @pl.when(h == 0)
-                def _():
-                    @pl.loop(0, CHUNKS)
-                    def _(q):
-                        for j in order:
-                            early(q, j).wait_recv()
-                        early_own(q).wait()
-
-                    second_start(halves + 1)
-            if c < halves:
-                pl.when(h > 0)(arrived)
-            else:
-                arrived()
-
-            @pl.when((g >= halves) & (g + 2 < groups))
-            def _():
-                second_start(g + 2)
-
-            @pl.when(z < zn - 1)
-            def _():
-                edge(g, True).start()
-
-            @pl.when(z > 0)
-            def _():
-                edge(g, False).start()
 
             @pl.loop(reach, nblk - reach)
             def _(i):
@@ -279,12 +286,18 @@
             for b in range(c):
                 gram(h, c * LANES, LANES, b)
             gram(h, 0, (c + 1) * LANES, c)
+            if c + 1 < cols:
+                take(g + 1, c + 1, False)
+            else:
+                @pl.when(h + 1 < slots)
+                def _():
+                    take(g + 1, 0, False)
             third_do(h, c, "start")
 
-        mine = pl.ds(pl.multiple_of(z * own_rows, own_rows), own_rows)
-        for c in range(cols):
-            out_k[h, :, c * LANES:(c + 1) * LANES] = g_f32[mine, c * 2 * LANES:c * 2 * LANES + LANES]
-            out_m[h, :, c * LANES:(c + 1) * LANES] = g_f32[mine, c * 2 * LANES + LANES:(c + 1) * 2 * LANES]
+        mine = pl.ds(pl.multiple_of(row_start(z), own_rows), own_rows)
+        for c in range(cols):
+            out_k[h, :, turn[c] * LANES:(turn[c] + 1) * LANES] = g_f32[mine, c * 2 * LANES:c * 2 * LANES + LANES]
+            out_m[h, :, turn[c] * LANES:(turn[c] + 1) * LANES] = g_f32[mine, c * 2 * LANES + LANES:(c + 1) * 2 * LANES]
 
     @pl.loop(0, slots)
     def _(h):
@@ -293,10 +306,11 @@
         for c in range(cols):
             for which, out in enumerate((out_k, out_m)):
                 start = (2 * c + which) * LANES
-                value = out[h, :, c * LANES:(c + 1) * LANES]
+                place_out = slice(turn[c] * LANES, (turn[c] + 1) * LANES)
+                value = out[h, :, place_out]
                 for j in range(1, zn):
                     value = value + g_recv[h, j - 1, :, start:start + LANES].astype(jnp.float32)
-                out[h, :, c * LANES:(c + 1) * LANES] = value
+                out[h, :, place_out] = value
 
     @pl.loop(0, CHUNKS)
     def _(q):

time: 176 us -> 147 us (0.84)
  Pallas kernels: 172 us -> 142 us
    pallas_call x1, Pallas kernels: 172 us -> 142 us  [per_device(): pl.pallas_call(functools.partial(kernel, (n, zn, sec, rows, modes, nblk,...]
where the time goes in v3:
time: 147 us
  Pallas kernels  142 us (97%)
  local copies, waits for them, and re-layouts  3.74 us (3%)
    pallas_call x1, Pallas kernels, per_device(): pl.pallas_call(functools.partial(kernel, (n, zn, sec, rows, modes, nblk,...  142 us
    unnamed x2, local copies, waits for them, and re-layouts  3.74 us

profile of v3, /device:TPU:24, one launch (start us, length us, event | category | flops | bytes accessed | tf_op | source)
XLA Modules:
  0.0 146.9 jit_solution(7509994317532972120)
XLA Ops:
  0.6 142.5 %shard_map.59 = (f32[2,128,512]{2,1,0:T(8,128)}, f32[2,128,512]{2,1,0:T(8,128)}) custom-call(s32[16]{0:T(128)} %table_ref.1, bf16[4,2048,256]{2,1,0:T(8,128)(2,1)} %psi_ref.1, bf16[16,5,128,128]{3,2,1,0:T(8,128)(2,1)} %stiff_ref.1, bf16[16,5,128,128]{3,2,1,0:T(8,128)(2,1)} %mass_ref.1), custom_call_target="tpu_custom_call" | custom-call | tf_op jit(solution)/shard_map/pallas_call | solution.py:359
  143.1 1.9 %copy.8 = f32[2,128,512]{2,1,0:T(8,128)} copy(f32[2,128,512]{2,1,0:T(8,128)} %get-tuple-element.4) | data formatting | bytes 1048576
  145.0 1.9 %copy.9 = f32[2,128,512]{2,1,0:T(8,128)} copy(f32[2,128,512]{2,1,0:T(8,128)} %get-tuple-element.5) | data formatting | bytes 1048576
